TPU v7x, 256 devices: a whole 4x4x8 slice. The times are simulated.
256 devices in a mesh: grid: 32 (over y, x, core), rows: 8 (over z).
Axes of the slice: x: 4, y: 4, z: 8, core: 2. Of those that a mesh axis runs over, the one named last changes fastest.
Arguments:
- density: bfloat16 [32, 128, 4096], P(None, 'rows', 'grid'), as said below
- basis_values: bfloat16 [64, 16, 128, 512], P('grid', None, 'rows'), may hold values from -0.59765625 to 0.59765625
- grid_points: float32 [64, 3, 512], P('grid'), may hold values from -4 to 4
- grid_weights: float32 [64, 512], P('grid'), may hold values from 0.05 to 1
- screened_blocks: int32 [64, 16], P('grid'), may hold values from 0 to 31, as said below
Outputs:
- exchange: float32 [32, 128, 4096], P(None, 'rows', 'grid')
Inputs may be any that keep to these rules, and one draw needn't show every extreme that they name: density is symmetric: density[a, i, b * 128 + j] equals density[b, j, a * 128 + i]. `screened_blocks`: each row holds 16 distinct block numbers.
All inputs are finite; a program needn't handle non-finite values.
Results may differ from a plain program's by a relative error of at most 0.00055.
The roundings to bfloat16 on the way count: a program that leaves them out, or rounds other values in their place, can miss the bound.
Values may be sent and summed in bfloat16 or wider, within the bound.
A program may use at most 64 MiB of HBM per device.

v0:
```python
import jax
import jax.numpy as jnp
from jax import lax
from jax.sharding import PartitionSpec as P


def copy_for_each(shard, axis):
    copies = jnp.broadcast_to(shard, (lax.axis_size(axis), *shard.shape))
    return lax.all_to_all(copies, axis, split_axis=0, concat_axis=0, tiled=True)


def joined_along(blocks, dim):
    shape = list(blocks.shape[1:])
    shape[dim] *= blocks.shape[0]
    return jnp.moveaxis(blocks, 0, dim).reshape(shape)


def gather_directly(shard, axis, dim):
    blocks = copy_for_each(shard, axis)
    return joined_along(blocks, dim)


def body(density, basis_values, grid_points, grid_weights, screened_blocks):
    nblocks = density.shape[0]
    rows_mine = density.shape[1]
    block_size = rows_mine * lax.axis_size("rows")
    nbasis = nblocks * block_size
    nsig = basis_values.shape[1]
    npoints = basis_values.shape[3]
    stripe = lax.all_gather(density, "grid", axis=2, tiled=True)
    totals = jnp.zeros((nblocks, rows_mine, nblocks, block_size), jnp.float32)
    for batch_index in range(basis_values.shape[0]):
        blocks = screened_blocks[batch_index]
        row_pick = jnp.take(stripe, blocks, axis=0).reshape(nsig * rows_mine, nblocks, block_size)
        chosen = jnp.take(row_pick, blocks, axis=1)
        local_values = basis_values[batch_index]
        x_mine = local_values.reshape(nsig * rows_mine, npoints)
        fsum = jnp.einsum(
            "mtk,tkp->mp",
            chosen,
            gather_directly(local_values, "rows", 1),
            preferred_element_type=jnp.float32,
        )
        fmat = fsum.astype(jnp.bfloat16)
        intersection_part = lax.dot_general(
            x_mine, fmat, (((0,), (0,)), ((), ())), preferred_element_type=jnp.float32
        )
        intersection = lax.psum(intersection_part, "rows")
        places = grid_points[batch_index]
        weights = grid_weights[batch_index]
        diffs = places[:, :, None] - places[:, None, :]
        kern = 1.0 / jnp.sqrt(jnp.sum(diffs * diffs, axis=0) + 0.5)
        mixed = (weights[:, None] * kern * intersection).astype(jnp.bfloat16)
        potential = (
            jnp.dot(x_mine, mixed, preferred_element_type=jnp.float32) * weights[None, :]
        ).astype(jnp.bfloat16)
        potential = potential.reshape(nsig, rows_mine, npoints)
        block_k = jnp.einsum(
            "mp,tkp->mtk",
            x_mine,
            lax.all_gather(potential, "rows", axis=1, tiled=True),
            preferred_element_type=jnp.float32,
        )
        block_k = block_k.reshape(nsig, rows_mine, nsig, block_size)
        totals = totals.at[blocks[:, None], :, blocks[None, :], :].add(
            block_k.transpose(0, 2, 1, 3)
        )
    return lax.psum_scatter(
        totals.reshape(nblocks, rows_mine, nbasis), "grid", scatter_dimension=2, tiled=True
    )


def solution(mesh):
    placed = (
        P(None, "rows", "grid"),
        P("grid", None, "rows", None),
        P("grid", None, None),
        P("grid", None),
        P("grid", None),
    )
    return jax.shard_map(
        body, mesh=mesh, in_specs=placed, out_specs=P(None, "rows", "grid"), check_vma=False
    )
```

profile of v0, /device:TPU:2, one launch (start us, length us, event | category | flops | bytes accessed | tf_op | source)
XLA Modules:
  0.0 494.6 jit_solution(1196830963108560420)
XLA Ops:
  8.6 59.6 %all_to_all.10 = bf16[8,16,16,512]{3,2,1,0:T(8,128)(2,1)} all-to-all(bf16[8,16,16,512]{3,2,1,0:T(8,128)(2,1)S(1)} %broadcast_in_dim.59), channel_id=1, replica_groups=mesh['grid'=32,'rows'=8] {'rows'}, dimensions={0} | all-to-all | bytes 4194304 | tf_op jit(solution)/shard_map/all_to_all | solution.py:9
  69.8 3.7 all-to-all-start
  73.7 3.2 copy.34
  76.8 46.5 %all-to-all-done = bf16[8,16,16,512]{3,2,1,0:T(8,128)(2,1)S(1)} async-done(((bf16[8,16,16,512]{3,2,1,0:T(8,128)(2,1)}), bf16[8,16,16,512]{3,2,1,0:T(8,128)(2,1)S(1)}, u32[]{:S(2)}, u32[]{:S(2)}) %all-to-all-start) | async-done | bytes 2097184 | tf_op jit(solution)/shard_map/all_to_all | solution.py:9
  124.9 2.9 gather_fusion.2
  131.1 2.9 gather_fusion
  137.2 4.1 convolution_bitcast_fusion.2
  141.3 3.3 convolution_bitcast_fusion.3
  146.0 77.3 %all-reduce.3.cloned.1.call-done = (f32[512,512]{0,1:T(8,128)}, f32[512,512]{0,1:T(8,128)}) async-done(((f32[512,512]{0,1:T(8,128)}, f32[512,512]{0,1:T(8,128)}), (f32[512,512]{0,1:T(8,128)}, f32[512,512]{0,1:T(8,128)})) %all-reduce.3.cloned.1.call-update) | async-done | bytes 2097168 | tf_op jit(solution)/shard_map/psum | solution.py:48
  223.3 2.3 fusion
  226.4 2.3 fusion.1
  229.3 36.4 %all-gather.6.cloned.1.call-done = bf16[16,128,512]{2,1,0:T(8,128)(2,1)} async-done(((bf16[16,16,512]{2,1,0:T(8,128)(2,1)}), bf16[16,128,512]{2,1,0:T(8,128)(2,1)}) %all-gather.6.cloned.1.call-update) | async-done | bytes 2097168 | tf_op jit(solution)/shard_map/all_gather | solution.py:61
  265.7 2.3 convolution_bitcast_fusion.1
  268.0 2.0 copy.30
  270.0 2.3 copy.31
  272.2 34.5 %all-gather.8.cloned.1.call-done = bf16[16,128,512]{2,1,0:T(8,128)(2,1)} async-done(((bf16[16,16,512]{2,1,0:T(8,128)(2,1)}), bf16[16,128,512]{2,1,0:T(8,128)(2,1)}) %all-gather.8.cloned.1.call-update) | async-done | bytes 2097168 | tf_op jit(solution)/shard_map/all_gather | solution.py:61
  306.8 3.6 convolution_bitcast_fusion
  310.4 3.1 copy.35
  313.5 3.6 copy.36
  317.1 4.2 broadcast_in_dim.51
  321.3 28.4 %scatter_fusion = f32[32,16,32,128]{3,1,2,0:T(8,128)} fusion(f32[32,16,32,128]{3,1,2,0:T(8,128)} %broadcast_in_dim.51, s32[256]{0:T(256)S(1)} %reshape.140, f32[256,16,128]{2,1,0:T(8,128)S(1)} %bitcast.107), kind=kCustom, calls=%fused_computation.4 | custom fusion | flops 524288 | bytes 6293504 | tf_op jit(solution)/shard_map/scatter-add | solution.py:65
  349.7 31.8 %scatter_fusion.1 = f32[32,16,32,128]{3,1,2,0:T(8,128)} fusion(f32[32,16,32,128]{3,1,2,0:T(8,128)} %scatter_fusion, s32[256]{0:T(256)S(1)} %reshape.146, f32[256,16,128]{2,1,0:T(8,128)} %bitcast.108), kind=kCustom, calls=%fused_computation.5 | custom fusion | flops 524288 | bytes 6293504 | tf_op jit(solution)/shard_map/scatter-add | solution.py:65
  381.5 7.8 %copy_bitcast_fusion = f32[32,16,4096]{2,1,0:T(8,128)} fusion(f32[32,16,32,128]{3,1,2,0:T(8,128)} %scatter_fusion.1), kind=kLoop, calls=%fused_computation.6 | loop fusion | bytes 16777216 | tf_op jit(solution)/shard_map/reshape | solution.py:69
  389.3 98.8 %reduce-scatter.2.cloned.1.call-done = f32[32,16,128]{2,1,0:T(8,128)} async-done(((f32[32,16,4096]{2,1,0:T(8,128)}), f32[32,16,128]{2,1,0:T(8,128)}) %reduce-scatter.2.cloned.1.call-update) | async-done | bytes 262160 | tf_op jit(solution)/shard_map/reduce_scatter | solution.py:68
  (49 shorter events, 14.5 us)
Async XLA Ops:
  6.5 118.4 %all-gather.4.cloned.1.call-start = ((), (), s32[]{:S(2)}) async-start(), calls=%async_computation.3 | async-start | bytes 4325376 | tf_op jit(solution)/shard_map/all_gather | solution.py:30
  69.8 3.8 copy-start.3
  69.8 53.5 %all-to-all-start = ((bf16[8,16,16,512]{3,2,1,0:T(8,128)(2,1)}), bf16[8,16,16,512]{3,2,1,0:T(8,128)(2,1)S(1)}, u32[]{:S(2)}, u32[]{:S(2)}) async-start(bf16[8,16,16,512]{3,2,1,0:T(8,128)(2,1)} %broadcast_in_dim.55), calls=%async_computation | async-start | bytes 4194304 | tf_op jit(solution)/shard_map/all_to_all | solution.py:9
  73.5 149.8 %all-reduce.3.cloned.1.call-start = ((), (), s32[]{:S(2)}) async-start(), calls=%async_computation.7 | async-start | bytes 4194304 | tf_op jit(solution)/shard_map/psum | solution.py:48
  137.2 4.1 copy-start
  144.6 0.7 copy-start.1
  144.6 1.4 copy-start.2
  144.6 121.1 %all-gather.6.cloned.1.call-start = ((), (), s32[]{:S(2)}) async-start(), calls=%async_computation.4 | async-start | bytes 2359296 | tf_op jit(solution)/shard_map/all_gather | solution.py:61
  225.7 81.1 %all-gather.8.cloned.1.call-start = ((), (), s32[]{:S(2)}) async-start(), calls=%async_computation.5 | async-start | bytes 2359296 | tf_op jit(solution)/shard_map/all_gather | solution.py:61
  228.7 259.3 %reduce-scatter.2.cloned.1.call-start = ((), (), s32[]{:S(2)}) async-start(), calls=%async_computation.6 | async-start | bytes 8650752 | tf_op jit(solution)/shard_map/reduce_scatter | solution.py:68
Sparse Core Ops, SparseCore 0:
  9.8 56.2 all-gather.3
  144.7 78.5 all-reduce.2
  225.8 39.8 all-gather.5
  267.3 39.4 all-gather.7
  389.4 98.5 reduce-scatter.1
where the time goes:
time: 496 us; the launch traced here: 495 us
  waiting for transfers between devices  294 us (59%)
  other arithmetic  61.6 us (12%)
  blocking collectives  59.6 us (12%)
  local copies, waits for them, and re-layouts  43.8 us (9%)
  matrix products  17.9 us (4%)
  between operations  13.4 us (3%)
    reduce_scatter x1, waiting for transfers between devices, body(): lax.psum_scatter(totals.reshape(nblocks, rows_mine, nbasis), 'grid', scat...  98.8 us
    psum x1, waiting for transfers between devices, body(): intersection = lax.psum(intersection_part, 'rows')  77.3 us
    all_gather x2, waiting for transfers between devices, body(): lax.all_gather(potential, 'rows', axis=1, tiled=True)  70.9 us
    scatter-add x2, other arithmetic, body(): totals.at[blocks[:, None], :, blocks[None, :], :]  60.2 us
    all_to_all x1, blocking collectives, copy_for_each(): return lax.all_to_all(copies, axis, split_axis=0, concat_axis=0, tiled=True)  59.6 us
    all_to_all x1, waiting for transfers between devices, copy_for_each(): return lax.all_to_all(copies, axis, split_axis=0, concat_axis=0, tiled=True)  46.5 us
  transfers between devices with their start and end apart: 6, of which 5 were waited for; matrix products, arithmetic and copies ran while one was open for 4% of the time, Pallas kernels for 0%

commit v1 on v0

--- a/solution.py
+++ b/solution.py
@@ -45,7 +45,7 @@
         intersection_part = lax.dot_general(
             x_mine, fmat, (((0,), (0,)), ((), ())), preferred_element_type=jnp.float32
         )
-        intersection = lax.psum(intersection_part, "rows")
+        intersection = jnp.sum(lax.all_gather(intersection_part, "rows"), axis=0)
         places = grid_points[batch_index]
         weights = grid_weights[batch_index]
         diffs = places[:, :, None] - places[:, None, :]

time: 496 us -> 587 us (1.18)
  waiting for transfers between devices: 294 us -> 404 us
  blocking collectives: 59.6 us -> 0 us
  local copies, waits for them, and re-layouts: 43.8 us -> 65 us
  starting transfers between devices: 4.08 us -> 13.3 us
  other arithmetic: 61.6 us -> 67.7 us
    all_gather x0 -> x2, waiting for transfers between devices: none -> 120 us  [body(): intersection = jnp.sum(lax.all_gather(intersection_part, 'rows'), axis=0)]
    all_to_all x1 -> x2, waiting for transfers between devices: 46.5 us -> 125 us  [copy_for_each(): return lax.all_to_all(copies, axis, split_axis=0, concat_axis=0, tiled=True)]
    psum x1 -> x0, waiting for transfers between devices: 77.3 us -> none  [body(): intersection = lax.psum(intersection_part, 'rows')]
    all_to_all x1 -> x0, blocking collectives: 59.6 us -> none  [copy_for_each(): return lax.all_to_all(copies, axis, split_axis=0, concat_axis=0, tiled=True)]
    unnamed x11 -> x13, local copies, waits for them, and re-layouts: 1.59 us -> 23.9 us
    all_gather x2, waiting for transfers between devices: 70.9 us -> 59.1 us  [body(): lax.all_gather(potential, 'rows', axis=1, tiled=True)]
    all_to_all x1 -> x2, starting transfers between devices: 3.73 us -> 12.2 us  [copy_for_each(): return lax.all_to_all(copies, axis, split_axis=0, concat_axis=0, tiled=True)]
    reduce_sum x0 -> x2, other arithmetic: none -> 6.11 us  [body(): intersection = jnp.sum(lax.all_gather(intersection_part, 'rows'), axis=0)]
  transfers between devices with their start and end apart: 6 -> 8, of which waited for: 5 -> 7; matrix products, arithmetic and copies ran while one was open for 4% -> 10% of each run, Pallas kernels for 0% -> 0%
where the time goes in v1:
time: 587 us; the launch traced here: 580 us
  waiting for transfers between devices  404 us (69%)
  other arithmetic  67.7 us (12%)
  local copies, waits for them, and re-layouts  65 us (11%)
  matrix products  16.8 us (3%)
  between operations  14 us (2%)
  starting transfers between devices  13.3 us (2%)
    all_to_all x2, waiting for transfers between devices, copy_for_each(): return lax.all_to_all(copies, axis, split_axis=0, concat_axis=0, tiled=True)  125 us
    all_gather x2, waiting for transfers between devices, body(): intersection = jnp.sum(lax.all_gather(intersection_part, 'rows'), axis=0)  120 us
    reduce_scatter x1, waiting for transfers between devices, body(): lax.psum_scatter(totals.reshape(nblocks, rows_mine, nbasis), 'grid', scat...  98.8 us
    scatter-add x2, other arithmetic, body(): totals.at[blocks[:, None], :, blocks[None, :], :]  60.2 us
    all_gather x2, waiting for transfers between devices, body(): lax.all_gather(potential, 'rows', axis=1, tiled=True)  59.1 us
    unnamed x13, local copies, waits for them, and re-layouts  23.9 us
    all_to_all x2, starting transfers between devices, copy_for_each(): return lax.all_to_all(copies, axis, split_axis=0, concat_axis=0, tiled=True)  12.2 us
  transfers between devices with their start and end apart: 8, of which 7 were waited for; matrix products, arithmetic and copies ran while one was open for 10% of the time, Pallas kernels for 0%

profile of v1, /device:TPU:2, one launch (start us, length us, event | category | flops | bytes accessed | tf_op | source)
XLA Modules:
  0.0 580.4 jit_solution(16691935981800096354)
XLA Ops:
  10.0 8.6 %all-to-all-start.1 = ((bf16[8,16,16,512]{3,2,1,0:T(8,128)(2,1)}), bf16[8,16,16,512]{3,2,1,0:T(8,128)(2,1)S(1)}, u32[]{:S(2)}, u32[]{:S(2)}) async-start(bf16[8,16,16,512]{3,2,1,0:T(8,128)(2,1)} %broadcast_in_dim.59), calls=%async_computation.1 | async-start | bytes 4194304 | tf_op jit(solution)/shard_map/all_to_all | solution.py:9
  18.7 51.1 %all-to-all-done.1 = bf16[8,16,16,512]{3,2,1,0:T(8,128)(2,1)S(1)} async-done(((bf16[8,16,16,512]{3,2,1,0:T(8,128)(2,1)}), bf16[8,16,16,512]{3,2,1,0:T(8,128)(2,1)S(1)}, u32[]{:S(2)}, u32[]{:S(2)}) %all-to-all-start.1) | async-done | bytes 2097184 | tf_op jit(solution)/shard_map/all_to_all | solution.py:9
  71.4 2.9 gather_fusion.2
  77.6 4.0 convolution_bitcast_fusion.2
  83.2 3.6 all-to-all-start
  86.8 73.9 %all-to-all-done = bf16[8,16,16,512]{3,2,1,0:T(8,128)(2,1)S(1)} async-done(((bf16[8,16,16,512]{3,2,1,0:T(8,128)(2,1)}), bf16[8,16,16,512]{3,2,1,0:T(8,128)(2,1)S(1)}, u32[]{:S(2)}, u32[]{:S(2)}) %all-to-all-start) | async-done | bytes 2097184 | tf_op jit(solution)/shard_map/all_to_all | solution.py:9
  162.3 2.9 gather_fusion
  167.6 3.7 convolution_bitcast_fusion.3
  172.2 42.7 %all-gather.16.cloned.1.call-done = f32[4096,512]{0,1:T(8,128)} async-done(((f32[512,512]{0,1:T(8,128)}), f32[4096,512]{0,1:T(8,128)}) %all-gather.16.cloned.1.call-update) | async-done | bytes 8388624 | tf_op jit(solution)/shard_map/all_gather | solution.py:48
  214.9 11.5 %copy.44 = f32[64,8,8,512]{3,2,1,0:T(8,128)S(1)} copy(f32[64,8,8,512]{3,1,2,0:T(8,128)} %bitcast.119) | data formatting | bytes 16777216
  226.4 3.1 bitcast_reduce_fusion
  232.5 77.3 %all-gather.14.cloned.1.call-done = f32[4096,512]{0,1:T(8,128)} async-done(((f32[512,512]{0,1:T(8,128)}), f32[4096,512]{0,1:T(8,128)}) %all-gather.14.cloned.1.call-update) | async-done | bytes 8388624 | tf_op jit(solution)/shard_map/all_gather | solution.py:48
  309.8 11.5 %copy.42 = f32[64,8,8,512]{3,2,1,0:T(8,128)S(1)} copy(f32[64,8,8,512]{3,1,2,0:T(8,128)} %bitcast.120) | data formatting | bytes 16777216
  321.3 3.1 bitcast_reduce_fusion.1
  326.4 24.8 %all-gather.12.cloned.1.call-done = bf16[16,128,512]{2,1,0:T(8,128)(2,1)} async-done(((bf16[16,16,512]{2,1,0:T(8,128)(2,1)}), bf16[16,128,512]{2,1,0:T(8,128)(2,1)}) %all-gather.12.cloned.1.call-update) | async-done | bytes 2097168 | tf_op jit(solution)/shard_map/all_gather | solution.py:61
  357.8 34.3 %all-gather.10.cloned.1.call-done = bf16[16,128,512]{2,1,0:T(8,128)(2,1)} async-done(((bf16[16,16,512]{2,1,0:T(8,128)(2,1)}), bf16[16,128,512]{2,1,0:T(8,128)(2,1)}) %all-gather.10.cloned.1.call-update) | async-done | bytes 2097168 | tf_op jit(solution)/shard_map/all_gather | solution.py:61
  392.1 3.6 convolution_bitcast_fusion.1
  395.7 3.1 copy.30
  398.8 3.6 copy.31
  402.4 4.2 broadcast_in_dim.51
  406.6 31.8 %scatter_fusion = f32[32,16,32,128]{3,1,2,0:T(8,128)} fusion(f32[32,16,32,128]{3,1,2,0:T(8,128)} %broadcast_in_dim.51, s32[256]{0:T(256)S(1)} %reshape.140, f32[256,16,128]{2,1,0:T(8,128)} %bitcast.118), kind=kCustom, calls=%fused_computation.4 | custom fusion | flops 524288 | bytes 6293504 | tf_op jit(solution)/shard_map/scatter-add | solution.py:65
  438.4 28.4 %scatter_fusion.1 = f32[32,16,32,128]{3,1,2,0:T(8,128)} fusion(f32[32,16,32,128]{3,1,2,0:T(8,128)} %scatter_fusion, s32[256]{0:T(256)S(1)} %reshape.146, f32[256,16,128]{2,1,0:T(8,128)S(1)} %bitcast.117), kind=kCustom, calls=%fused_computation.5 | custom fusion | flops 524288 | bytes 6293504 | tf_op jit(solution)/shard_map/scatter-add | solution.py:65
  466.8 7.8 %copy_bitcast_fusion = f32[32,16,4096]{2,1,0:T(8,128)} fusion(f32[32,16,32,128]{3,1,2,0:T(8,128)} %scatter_fusion.1), kind=kLoop, calls=%fused_computation.8 | loop fusion | bytes 16777216 | tf_op jit(solution)/shard_map/reshape | solution.py:69
  474.6 98.8 %reduce-scatter.2.cloned.1.call-done = f32[32,16,128]{2,1,0:T(8,128)} async-done(((f32[32,16,4096]{2,1,0:T(8,128)}), f32[32,16,128]{2,1,0:T(8,128)}) %reduce-scatter.2.cloned.1.call-update) | async-done | bytes 262160 | tf_op jit(solution)/shard_map/reduce_scatter | solution.py:68
  (57 shorter events, 26.4 us)
Async XLA Ops:
  6.5 64.9 %all-gather.8.cloned.1.call-start = ((), (), s32[]{:S(2)}) async-start(), calls=%async_computation.3 | async-start | bytes 4325376 | tf_op jit(solution)/shard_map/all_gather | solution.py:30
  8.4 69.2 %copy-start = (bf16[1,16,16,512]{3,2,1,0:T(8,128)(2,1)}, bf16[1,16,16,512]{3,2,1,0:T(8,128)(2,1)S(1)}, u32[]{:S(2)}) copy-start(bf16[1,16,16,512]{3,2,1,0:T(8,128)(2,1)S(1)} %get-tuple-element.13) | copy-start | bytes 786436
  10.0 8.6 %copy-start.3 = (s32[2,16]{1,0:T(2,128)S(1)}, s32[2,16]{1,0:T(2,128)}, u32[]{:S(2)}) copy-start(s32[2,16]{1,0:T(2,128)} %param.13) | copy-start | bytes 388
  10.0 59.8 %all-to-all-start.1 = ((bf16[8,16,16,512]{3,2,1,0:T(8,128)(2,1)}), bf16[8,16,16,512]{3,2,1,0:T(8,128)(2,1)S(1)}, u32[]{:S(2)}, u32[]{:S(2)}) async-start(bf16[8,16,16,512]{3,2,1,0:T(8,128)(2,1)} %broadcast_in_dim.59), calls=%async_computation.1 | async-start | bytes 4194304 | tf_op jit(solution)/shard_map/all_to_all | solution.py:9
  18.6 196.3 %all-gather.16.cloned.1.call-start = ((), (), s32[]{:S(2)}) async-start(), calls=%async_computation.8 | async-start | bytes 9437184 | tf_op jit(solution)/shard_map/all_gather | solution.py:48
  83.2 77.6 %all-to-all-start = ((bf16[8,16,16,512]{3,2,1,0:T(8,128)(2,1)}), bf16[8,16,16,512]{3,2,1,0:T(8,128)(2,1)S(1)}, u32[]{:S(2)}, u32[]{:S(2)}) async-start(bf16[8,16,16,512]{3,2,1,0:T(8,128)(2,1)} %broadcast_in_dim.55), calls=%async_computation | async-start | bytes 4194304 | tf_op jit(solution)/shard_map/all_to_all | solution.py:9
  86.8 223.1 %all-gather.14.cloned.1.call-start = ((), (), s32[]{:S(2)}) async-start(), calls=%async_computation.7 | async-start | bytes 9437184 | tf_op jit(solution)/shard_map/all_gather | solution.py:48
  167.6 4.3 copy-start.1
  171.3 1.0 copy-start.2
  171.3 179.9 %all-gather.12.cloned.1.call-start = ((), (), s32[]{:S(2)}) async-start(), calls=%async_computation.5 | async-start | bytes 2359296 | tf_op jit(solution)/shard_map/all_gather | solution.py:61
  231.9 160.2 %all-gather.10.cloned.1.call-start = ((), (), s32[]{:S(2)}) async-start(), calls=%async_computation.4 | async-start | bytes 2359296 | tf_op jit(solution)/shard_map/all_gather | solution.py:61
  325.8 247.5 %reduce-scatter.2.cloned.1.call-start = ((), (), s32[]{:S(2)}) async-start(), calls=%async_computation.6 | async-start | bytes 8650752 | tf_op jit(solution)/shard_map/reduce_scatter | solution.py:68
Sparse Core Ops, SparseCore 0:
  9.8 56.2 all-gather.7
  81.7 133.1 all-gather.15
  216.7 93.0 all-gather.13
  311.5 39.7 all-gather.11
  352.9 39.1 all-gather.9
  474.7 98.5 reduce-scatter.1
